TPU v7x, 32 devices: a whole 2x2x4 slice. The times are simulated.
32 devices in a mesh: tm: 2 (over x), chan: 4 (over y, core), bl: 4 (over z).
Axes of the slice: x: 2, y: 2, z: 4, core: 2. Of those that a mesh axis runs over, the one named last changes fastest.
Arguments:
- voltages: bfloat16 [2, 256, 128, 512], P(None, ('chan', 'bl'), None, 'tm'), may hold values from -6 to 6
Outputs:
- visibilities: bfloat16 [2, 128, 4, 256, 256], P(None, ('chan', 'bl'), 'tm')
All inputs are finite; a program needn't handle non-finite values.
Results may differ from a plain program's by a relative error of at most 0.0051.
Values may be sent and summed in bfloat16 or wider, within the bound.
No kernel may reach another device: no remote copies, remote signals or barrier semaphores. Data moves between devices by JAX's collectives and lax.ppermute only.
A program may use at most 64 MiB of HBM per device.

v0:
```python
import jax
import jax.numpy as jnp
from jax import lax
from jax.sharding import PartitionSpec as P

HALF = 128


def passed_along(block, axis, distance):
    devices = range(lax.axis_size(axis))
    route = [(i - distance, i) for i in devices if i - distance in devices]
    return lax.ppermute(block, axis, route)


def tapers(length):
    steps = jnp.arange(length, dtype=jnp.float32)
    taper_early = jnp.sin(jnp.pi * (steps + 0.5) / (2.0 * length))
    taper_late = jnp.sin(jnp.pi * (steps + 0.5 + length) / (2.0 * length))
    return (taper_early, taper_late)


def weighted(block, taper):
    return (block.astype(jnp.float32) * taper).astype(jnp.bfloat16)


def products(stacked):
    signals = stacked.shape[0] // 2
    gram = jnp.einsum("pct,qct->cpq", stacked, stacked, preferred_element_type=jnp.float32)
    real_part = gram[:, :signals, :signals] + gram[:, signals:, signals:]
    imag_part = gram[:, signals:, :signals] - gram[:, :signals, signals:]
    return (real_part, imag_part)


def local(voltages):
    turned = lax.all_to_all(voltages, ("chan", "bl"), split_axis=2, concat_axis=1, tiled=True)
    signals = turned.shape[1]
    channels = turned.shape[2]
    samples = turned.shape[3]
    halves = samples // HALF
    scale = 1.0 / HALF
    taper_early, taper_late = tapers(HALF)
    stacked = turned.reshape(2 * signals, channels, samples)
    lates = []
    earlies = []
    for index in range(halves):
        piece = stacked[:, :, index * HALF : (index + 1) * HALF]
        lates.append(products(weighted(piece, taper_late)))
        if index + 1 < halves:
            earlies.append(products(weighted(piece, taper_early)))
    tail = turned[:, :, :, samples - HALF :]
    received = passed_along(tail, "tm", 1)
    previous = products(weighted(received.reshape(2 * signals, channels, HALF), taper_early))
    real_list = []
    imag_list = []
    for index in range(halves):
        late_real, late_imag = lates[index]
        real_list.append(((late_real + previous[0]) * scale).astype(jnp.bfloat16))
        imag_list.append(((late_imag + previous[1]) * scale).astype(jnp.bfloat16))
        if index + 1 < halves:
            previous = earlies[index]
    return jnp.stack([jnp.stack(real_list, 1), jnp.stack(imag_list, 1)], 0)


def solution(mesh):
    return jax.shard_map(
        local,
        mesh=mesh,
        in_specs=(P(None, ("chan", "bl"), None, "tm"),),
        out_specs=P(None, ("chan", "bl"), "tm", None, None),
        check_vma=False,
    )
```

profile of v0, /device:TPU:0, one launch (start us, length us, event | category | flops | bytes accessed | tf_op | source)
XLA Modules:
  0.0 100.2 jit_solution(14008793336782749242)
XLA Ops:
  0.0 2.8 %copy.22 = bf16[2,16,128,256]{3,1,0,2:T(8,128)(2,1)S(1)} copy(bf16[2,16,128,256]{3,2,1,0:T(8,128)(2,1)} %param.1) | data formatting | bytes 4194304 | tf_op args[0]
  2.8 56.5 %all_to_all.18 = bf16[2,16,128,256]{3,1,0,2:T(8,128)(2,1)S(1)} all-to-all(bf16[2,16,128,256]{3,1,0,2:T(8,128)(2,1)S(1)} %copy.22), channel_id=1, replica_groups=mesh['tm'=2,'chan'=4,'bl'=4] {'chan','bl'}, dimensions={2} | all-to-all | bytes 4194304 | tf_op jit(solution)/shard_map/all_to_all | solution.py:35
  59.3 1.7 %copy.24 = bf16[2,16,16,8,256]{4,3,2,1,0:T(8,128)(2,1)S(1)} copy(bf16[2,16,16,8,256]{4,2,0,3,1:T(8,128)(2,1)S(1)} %bitcast.24) | data formatting | bytes 4194304 | tf_op jit(solution)/shard_map/all_to_all | solution.py:35
  61.0 0.1 slice.79
  61.1 3.6 %collective-permute-start = (bf16[2,256,8,128]{3,2,1,0:T(8,128)(2,1)S(1)}, bf16[2,256,8,128]{3,2,1,0:T(8,128)(2,1)S(1)}, u32[]{:S(2)}, u32[]{:S(2)}) collective-permute-start(bf16[2,256,8,128]{3,2,1,0:T(8,128)(2,1)S(1)} %slice.79), channel_id=1, source_target_pairs={{0,16},{1,17},{2,18},{3,19},{4,20},{5,21},{6,22},{7,23},{8,24},{9,... | collective-permute-start | bytes 3145736 | tf_op jit(solution)/shard_map/ppermute | solution.py:12
  64.7 0.1 multiply_sine_fusion
  64.8 22.0 %collective-permute-done = bf16[2,256,8,128]{3,2,1,0:T(8,128)(2,1)S(1)} collective-permute-done((bf16[2,256,8,128]{3,2,1,0:T(8,128)(2,1)S(1)}, bf16[2,256,8,128]{3,2,1,0:T(8,128)(2,1)S(1)}, u32[]{:S(2)}, u32[]{:S(2)}) %collective-permute-start) | collective-permute-done | bytes 1048608 | tf_op jit(solution)/shard_map/ppermute | solution.py:12
  86.8 0.8 fusion
  87.7 1.3 %fusion.23 = f32[8,512,512]{2,1,0:T(8,128)S(1)} fusion(bf16[512,8,128]{2,1,0:T(8,128)(2,1)S(1)} %get-tuple-element.12), kind=kOutput, calls=%fused_computation.38 | convolution fusion | flops 536870912 | bytes 9437184 | tf_op jit(solution)/shard_map/pct,qct->cpq/dot_general | solution.py:28
  88.9 1.3 %fusion.25 = f32[8,512,512]{2,1,0:T(8,128)S(1)} fusion(bf16[512,8,128]{2,1,0:T(8,128)(2,1)S(1)} %get-tuple-element.9), kind=kOutput, calls=%fused_computation.40 | convolution fusion | flops 536870912 | bytes 9437184 | tf_op jit(solution)/shard_map/pct,qct->cpq/dot_general | solution.py:28
  90.2 1.3 %fusion.19 = f32[8,512,512]{2,1,0:T(8,128)S(1)} fusion(bf16[512,8,128]{2,1,0:T(8,128)(2,1)S(1)} %get-tuple-element.11), kind=kOutput, calls=%fused_computation.34 | convolution fusion | flops 536870912 | bytes 9437184 | tf_op jit(solution)/shard_map/pct,qct->cpq/dot_general | solution.py:28
  91.5 1.3 %fusion.21 = f32[8,512,512]{2,1,0:T(8,128)S(1)} fusion(bf16[512,8,128]{2,1,0:T(8,128)(2,1)S(1)} %get-tuple-element.10), kind=kOutput, calls=%fused_computation.36 | convolution fusion | flops 536870912 | bytes 9437184 | tf_op jit(solution)/shard_map/pct,qct->cpq/dot_general | solution.py:28
  92.7 2.2 %fusion.15 = (bf16[8,1,256,256]{3,2,0,1:T(8,128)(2,1)S(1)}, bf16[8,1,256,256]{3,2,0,1:T(8,128)(2,1)S(1)}) fusion(f32[8,512,512]{2,1,0:T(8,128)S(1)} %fusion.23, f32[8,512,512]{2,1,0:T(8,128)S(1)} %fusion.25), kind=kLoop, calls=%fused_computation.30 | loop fusion | flops 5242880 | bytes 18874368 | tf_op jit(solution)/shard_map/stack | solution.py:61
  94.9 2.2 %fusion.16 = (bf16[8,1,256,256]{3,2,0,1:T(8,128)(2,1)S(1)}, bf16[8,1,256,256]{3,2,0,1:T(8,128)(2,1)S(1)}) fusion(f32[8,512,512]{2,1,0:T(8,128)S(1)} %fusion.19, f32[8,512,512]{2,1,0:T(8,128)S(1)} %fusion.21), kind=kLoop, calls=%fused_computation.31 | loop fusion | flops 5242880 | bytes 18874368 | tf_op jit(solution)/shard_map/stack | solution.py:61
  97.2 0.2 maximum_bitcast_fusion
  97.4 0.2 maximum_bitcast_fusion.1
  97.6 0.4 pad_maximum_fusion
  98.0 2.3 %copy.34 = bf16[2,8,2,256,256]{4,3,2,1,0:T(8,128)(2,1)} copy(bf16[2,8,2,256,256]{4,3,1,2,0:T(8,128)(2,1)S(1)} %pad_maximum_fusion) | data formatting | bytes 8388608 | tf_op jit(solution)/shard_map/stack | solution.py:61
Async XLA Ops:
  61.1 25.8 %collective-permute-start = (bf16[2,256,8,128]{3,2,1,0:T(8,128)(2,1)S(1)}, bf16[2,256,8,128]{3,2,1,0:T(8,128)(2,1)S(1)}, u32[]{:S(2)}, u32[]{:S(2)}) collective-permute-start(bf16[2,256,8,128]{3,2,1,0:T(8,128)(2,1)S(1)} %slice.79), channel_id=1, source_target_pairs={{0,16},{1,17},{2,18},{3,19},{4,20},{5,21},{6,22},{7,23},{8,24},{9,... | collective-permute-start | bytes 3145736 | tf_op jit(solution)/shard_map/ppermute | solution.py:12
where the time goes:
time: 100 us
  blocking collectives  56.5 us (56%)
  waiting for transfers between devices  22 us (22%)
  local copies, waits for them, and re-layouts  6.84 us (7%)
  other arithmetic  6.05 us (6%)
  matrix products  5.05 us (5%)
  starting transfers between devices  3.64 us (4%)
    all_to_all x1, blocking collectives, local(): lax.all_to_all(voltages, ('chan', 'bl'), split_axis=2, concat_axis=1, til...  56.5 us
    ppermute x1, waiting for transfers between devices, passed_along(): return lax.ppermute(block, axis, route)  22 us
    another operation x5, other arithmetic, local(): return jnp.stack([jnp.stack(real_list, 1), jnp.stack(imag_list, 1)], 0)  5.19 us
    dot_general x4, matrix products, products(): jnp.einsum('pct,qct->cpq', stacked, stacked, preferred_element_type=jnp.f...  5.05 us
    ppermute x1, starting transfers between devices, passed_along(): return lax.ppermute(block, axis, route)  3.64 us
    unnamed x1, local copies, waits for them, and re-layouts  2.76 us
    another operation x1, local copies, waits for them, and re-layouts, local(): return jnp.stack([jnp.stack(real_list, 1), jnp.stack(imag_list, 1)], 0)  2.29 us
  transfers between devices with their start and end apart: 1, of which 1 were waited for; matrix products, arithmetic and copies ran while one was open for 0% of the time, Pallas kernels for 0%

commit v1 on v0

v1 whole, which is shorter than its diff:
```python
import functools

import jax
import jax.numpy as jnp
from jax import lax
from jax.experimental import pallas as pl
from jax.experimental.pallas import tpu as pltpu
from jax.sharding import PartitionSpec as P

HALF = 128
ROWS = 16


def passed_along(block, axis, distance):
    devices = range(lax.axis_size(axis))
    route = [(i - distance, i) for i in devices if i - distance in devices]
    return lax.ppermute(block, axis, route)


def tapers(length):
    steps = jnp.arange(length, dtype=jnp.float32)
    taper_early = jnp.sin(jnp.pi * (steps + 0.5) / (2.0 * length))
    taper_late = jnp.sin(jnp.pi * (steps + 0.5 + length) / (2.0 * length))
    return jnp.stack([taper_early, taper_late])


def turned(piece):
    parts, signals, channels, samples = piece.shape
    devices = lax.axis_size("chan") * lax.axis_size("bl")
    by_channel = jnp.transpose(piece, (2, 0, 1, 3))
    swapped = lax.all_to_all(by_channel, ("chan", "bl"), split_axis=0, concat_axis=0, tiled=True)
    swapped = swapped.reshape(devices, channels // devices, parts, signals, samples)
    if signals % ROWS:
        swapped = jnp.transpose(swapped, (1, 2, 0, 3, 4))
        swapped = swapped.reshape(1, channels // devices, parts, devices * signals, samples)
    return swapped


def correlate(taper_ref, *refs):
    blocks, out_ref = refs[:-1], refs[-1]
    taper_early, taper_late = taper_ref[0:1, :], taper_ref[1:2, :]
    scale = 1.0 / HALF

    def part(block, index, taper):
        values = block[:, 0, index]
        values = values.reshape(values.shape[0] * values.shape[1], values.shape[2])
        return (values.astype(jnp.float32) * taper).astype(jnp.bfloat16)

    for window in range(len(blocks) - 1):
        late_a, late_b = (part(blocks[window + 1], i, taper_late) for i in range(2))
        early_a, early_b = (part(blocks[window], i, taper_early) for i in range(2))
        straight = jnp.concatenate([late_a, late_b, early_a, early_b], axis=1)
        crossed = jnp.concatenate([late_b, -late_a, early_b, -early_a], axis=1)
        for index, left in enumerate((straight, crossed)):
            gram = lax.dot_general(left, straight, (((1,), (1,)), ((), ())), preferred_element_type=jnp.float32)
            out_ref[index, 0, window] = (gram * scale).astype(jnp.bfloat16)


def correlated(blocks):
    sources, channels, parts, signals, samples = blocks[0].shape
    windows = len(blocks) - 1
    everyone = sources * signals
    spec = pl.BlockSpec((sources, 1, parts, signals, samples), lambda c: (0, c, 0, 0, 0))
    flops = channels * windows * 2 * parts * everyone * everyone * 2 * parts * samples
    return pl.pallas_call(
        correlate,
        grid=(channels,),
        in_specs=[pl.BlockSpec((2, samples), lambda c: (0, 0))] + [spec] * len(blocks),
        out_specs=pl.BlockSpec((parts, 1, windows, everyone, everyone), lambda c: (0, c, 0, 0, 0)),
        out_shape=jax.ShapeDtypeStruct((parts, channels, windows, everyone, everyone), jnp.bfloat16),
        cost_estimate=pl.CostEstimate(flops=flops, bytes_accessed=8 << 20, transcendentals=0),
        name="correlate",
    )(tapers(samples), *blocks)


def local(voltages):
    halves = voltages.shape[3] // HALF
    pieces = [voltages[:, :, :, i * HALF : (i + 1) * HALF] for i in range(halves)]
    last = turned(pieces[-1])
    received = passed_along(last, "tm", 1)
    blocks = [received]
    for piece in pieces[:-1]:
        piece, last = lax.optimization_barrier((piece, last))
        blocks.append(turned(piece))
    return correlated(blocks + [last])


def solution(mesh):
    return jax.shard_map(
        local,
        mesh=mesh,
        in_specs=(P(None, ("chan", "bl"), None, "tm"),),
        out_specs=P(None, ("chan", "bl"), "tm", None, None),
        check_vma=False,
    )
```

time: 100 us -> 77.6 us (0.78)
  blocking collectives: 56.5 us -> 0 us
  waiting for transfers between devices: 22 us -> 47.9 us
  starting transfers between devices: 3.64 us -> 14.5 us
  Pallas kernels: 0 us -> 8.08 us
  other arithmetic: 6.05 us -> 0.63 us
  matrix products: 5.05 us -> 0 us
    all_to_all x1 -> x0, blocking collectives: 56.5 us -> none  [local(): lax.all_to_all(voltages, ('chan', 'bl'), split_axis=2, concat_axis=1, til...]
    all_to_all x0 -> x2, waiting for transfers between devices: none -> 25.7 us  [turned(): lax.all_to_all(by_channel, ('chan', 'bl'), split_axis=0, concat_axis=0, t...]
    all_to_all x0 -> x2, starting transfers between devices: none -> 11.1 us  [turned(): lax.all_to_all(by_channel, ('chan', 'bl'), split_axis=0, concat_axis=0, t...]
    pallas_call x0 -> x1, Pallas kernels: none -> 8.08 us  [correlated(): pl.pallas_call(correlate, grid=(channels,), in_specs=[pl.BlockSpec((2, sa...]
    dot_general x4 -> x0, matrix products: 5.05 us -> none  [products(): jnp.einsum('pct,qct->cpq', stacked, stacked, preferred_element_type=jnp.f...]
    another operation x5 -> x1, other arithmetic: 5.19 us -> 0.57 us  [tapers(): return jnp.stack([taper_early, taper_late])]
    another operation x1 -> x0, local copies, waits for them, and re-layouts: 2.29 us -> none  [local(): return jnp.stack([jnp.stack(real_list, 1), jnp.stack(imag_list, 1)], 0)]
    all_to_all x1 -> x0, local copies, waits for them, and re-layouts: 1.72 us -> none  [local(): lax.all_to_all(voltages, ('chan', 'bl'), split_axis=2, concat_axis=1, til...]
  transfers between devices with their start and end apart: 1 -> 3, of which waited for: 1 -> 3; matrix products, arithmetic and copies ran while one was open for 0% -> 3% of each run, Pallas kernels for 0% -> 0%
where the time goes in v1:
time: 77.6 us; the launch traced here: 77.1 us
  waiting for transfers between devices  47.9 us (62%)
  starting transfers between devices  14.5 us (19%)
  Pallas kernels  8.08 us (10%)
  local copies, waits for them, and re-layouts  5.96 us (8%)
    all_to_all x2, waiting for transfers between devices, turned(): lax.all_to_all(by_channel, ('chan', 'bl'), split_axis=0, concat_axis=0, t...  25.7 us
    ppermute x1, waiting for transfers between devices, passed_along(): return lax.ppermute(block, axis, route)  22.2 us
    all_to_all x2, starting transfers between devices, turned(): lax.all_to_all(by_channel, ('chan', 'bl'), split_axis=0, concat_axis=0, t...  11.1 us
    pallas_call x1, Pallas kernels, correlated(): pl.pallas_call(correlate, grid=(channels,), in_specs=[pl.BlockSpec((2, sa...  8.08 us
    ppermute x1, starting transfers between devices, passed_along(): return lax.ppermute(block, axis, route)  3.46 us
    unnamed x7, local copies, waits for them, and re-layouts  2.63 us
    slice x1, local copies, waits for them, and re-layouts, local(): pieces = [voltages[:, :, :, i * HALF:(i + 1) * HALF] for i in range(halves)]  1.68 us
    optimization_barrier x1, local copies, waits for them, and re-layouts, local(): piece, last = lax.optimization_barrier((piece, last))  1.66 us
  transfers between devices with their start and end apart: 3, of which 3 were waited for; matrix products, arithmetic and copies ran while one was open for 3% of the time, Pallas kernels for 0%

profile of v1, /device:TPU:0, one launch (start us, length us, event | category | flops | bytes accessed | tf_op | source)
XLA Modules:
  0.0 77.1 jit_solution(1231677530440321354)
XLA Ops:
  0.0 1.7 %fusion = (bf16[2,16,128,128]{3,2,1,0:T(8,128)(2,1)S(1)}, bf16[2,16,128,128]{3,2,1,0:T(8,128)(2,1)S(1)}) fusion(bf16[2,16,128,256]{3,2,1,0:T(8,128)(2,1)} %param.1), kind=kLoop, calls=%fused_computation.4 | loop fusion | bytes 4194304 | tf_op jit(solution)/shard_map/slice | solution.py:78
  1.7 1.6 %copy.9 = bf16[2,16,128,128]{3,1,0,2:T(8,128)(2,1)} copy(bf16[2,16,128,128]{3,2,1,0:T(8,128)(2,1)S(1)} %get-tuple-element.10) | data formatting | bytes 2097152
  3.3 7.4 %all-to-all-start = ((bf16[128,2,16,128]{3,2,1,0:T(8,128)(2,1)}), bf16[128,2,16,128]{3,2,1,0:T(8,128)(2,1)S(1)}, u32[]{:S(2)}, u32[]{:S(2)}) async-start(bf16[128,2,16,128]{3,2,1,0:T(8,128)(2,1)} %bitcast.5), calls=%async_computation | async-start | bytes 2097152 | tf_op jit(solution)/shard_map/all_to_all | solution.py:31
  10.8 1.7 %copy.7 = bf16[2,16,128,128]{3,1,0,2:T(8,128)(2,1)} copy(bf16[2,16,128,128]{3,2,1,0:T(8,128)(2,1)S(1)} %get-tuple-element.9) | data formatting | bytes 2097152 | tf_op jit(solution)/shard_map/optimization_barrier | solution.py:83
  12.4 25.2 %all-to-all-done = bf16[128,2,16,128]{3,2,1,0:T(8,128)(2,1)S(1)} async-done(((bf16[128,2,16,128]{3,2,1,0:T(8,128)(2,1)}), bf16[128,2,16,128]{3,2,1,0:T(8,128)(2,1)S(1)}, u32[]{:S(2)}, u32[]{:S(2)}) %all-to-all-start) | async-done | bytes 1048608 | tf_op jit(solution)/shard_map/all_to_all | solution.py:31
  37.6 0.0 copy-start
  37.6 3.7 %all-to-all-start.1 = ((bf16[128,2,16,128]{3,2,1,0:T(8,128)(2,1)}), bf16[128,2,16,128]{3,2,1,0:T(8,128)(2,1)S(1)}, u32[]{:S(2)}, u32[]{:S(2)}) async-start(bf16[128,2,16,128]{3,2,1,0:T(8,128)(2,1)} %bitcast.2), calls=%async_computation.1 | async-start | bytes 2097152 | tf_op jit(solution)/shard_map/all_to_all | solution.py:31
  41.3 3.5 %collective-permute-start = (bf16[16,8,2,16,128]{4,3,2,1,0:T(8,128)(2,1)S(1)}, bf16[16,8,2,16,128]{4,3,2,1,0:T(8,128)(2,1)S(1)}, u32[]{:S(2)}, u32[]{:S(2)}) collective-permute-start(bf16[16,8,2,16,128]{4,3,2,1,0:T(8,128)(2,1)S(1)} %bitcast.6), channel_id=1, source_target_pairs={{0,16},{1,17},{2,18},{3,19},{4,20},{5,21},{6,22},{7,23},{8,24},{9,... | collective-permute-start | bytes 3145736 | tf_op jit(solution)/shard_map/ppermute | solution.py:17
  44.7 0.1 multiply_sine_fusion
  44.8 0.6 pad_maximum_fusion.taper_ref
  45.4 22.2 %collective-permute-done.refs_0_ = bf16[16,8,2,16,128]{4,3,2,1,0:T(8,128)(2,1)S(1)} collective-permute-done((bf16[16,8,2,16,128]{4,3,2,1,0:T(8,128)(2,1)S(1)}, bf16[16,8,2,16,128]{4,3,2,1,0:T(8,128)(2,1)S(1)}, u32[]{:S(2)}, u32[]{:S(2)}) %collective-permute-start) | collective-permute-done | bytes 1048608 | tf_op jit(solution)/shard_map/ppermute | solution.py:17
  67.5 0.0 copy-start.2
  67.5 0.6 all-to-all-done.1
  68.1 0.0 copy-start.1
  68.1 0.0 copy-done
  68.1 0.4 copy-done.2
  68.5 0.6 copy-done.1
  69.1 8.1 %correlate.1 = bf16[2,8,2,256,256]{4,3,2,1,0:T(8,128)(2,1)} custom-call(f32[2,128]{1,0:T(2,128)} %pad_maximum_fusion.taper_ref, bf16[16,8,2,16,128]{4,3,2,1,0:T(8,128)(2,1)} %copy-done.2, bf16[16,8,2,16,128]{4,3,2,1,0:T(8,128)(2,1)} %bitcast.8, bf16[16,8,2,16,128]{4,3,2,1,0:T(8,128)(2,1)} %bitcast.7), custom_call_target="tpu_custom_call" | custom-call | flops 2147483648 | bytes 8388608 | tf_op jit(solution)/shard_map/correlate/pallas_call | solution.py:65
Async XLA Ops:
  3.3 34.3 %all-to-all-start = ((bf16[128,2,16,128]{3,2,1,0:T(8,128)(2,1)}), bf16[128,2,16,128]{3,2,1,0:T(8,128)(2,1)S(1)}, u32[]{:S(2)}, u32[]{:S(2)}) async-start(bf16[128,2,16,128]{3,2,1,0:T(8,128)(2,1)} %bitcast.5), calls=%async_computation | async-start | bytes 2097152 | tf_op jit(solution)/shard_map/all_to_all | solution.py:31
  37.6 30.5 %copy-start = (bf16[128,2,16,128]{3,2,1,0:T(8,128)(2,1)}, bf16[128,2,16,128]{3,2,1,0:T(8,128)(2,1)S(1)}, u32[]{:S(2)}) copy-start(bf16[128,2,16,128]{3,2,1,0:T(8,128)(2,1)S(1)} %all-to-all-done) | copy-start | bytes 3145732
  37.6 30.5 %all-to-all-start.1 = ((bf16[128,2,16,128]{3,2,1,0:T(8,128)(2,1)}), bf16[128,2,16,128]{3,2,1,0:T(8,128)(2,1)S(1)}, u32[]{:S(2)}, u32[]{:S(2)}) async-start(bf16[128,2,16,128]{3,2,1,0:T(8,128)(2,1)} %bitcast.2), calls=%async_computation.1 | async-start | bytes 2097152 | tf_op jit(solution)/shard_map/all_to_all | solution.py:31
  41.3 26.3 %collective-permute-start = (bf16[16,8,2,16,128]{4,3,2,1,0:T(8,128)(2,1)S(1)}, bf16[16,8,2,16,128]{4,3,2,1,0:T(8,128)(2,1)S(1)}, u32[]{:S(2)}, u32[]{:S(2)}) collective-permute-start(bf16[16,8,2,16,128]{4,3,2,1,0:T(8,128)(2,1)S(1)} %bitcast.6), channel_id=1, source_target_pairs={{0,16},{1,17},{2,18},{3,19},{4,20},{5,21},{6,22},{7,23},{8,24},{9,... | collective-permute-start | bytes 3145736 | tf_op jit(solution)/shard_map/ppermute | solution.py:17
  67.5 1.0 %copy-start.2 = (bf16[16,8,2,16,128]{4,3,2,1,0:T(8,128)(2,1)}, bf16[16,8,2,16,128]{4,3,2,1,0:T(8,128)(2,1)S(1)}, u32[]{:S(2)}) copy-start(bf16[16,8,2,16,128]{4,3,2,1,0:T(8,128)(2,1)S(1)} %collective-permute-done.refs_0_) | copy-start | bytes 3145732
  68.1 1.0 %copy-start.1 = (bf16[128,2,16,128]{3,2,1,0:T(8,128)(2,1)}, bf16[128,2,16,128]{3,2,1,0:T(8,128)(2,1)S(1)}, u32[]{:S(2)}) copy-start(bf16[128,2,16,128]{3,2,1,0:T(8,128)(2,1)S(1)} %all-to-all-done.1) | copy-start | bytes 3145732
